TPU v7x, 32 devices: a whole 2x2x4 slice. The times are simulated.
32 devices in a mesh: gx: 4 (over x, core), gy: 8 (over z, y).
Axes of the slice: x: 2, y: 2, z: 4, core: 2. Of those that a mesh axis runs over, the one named last changes fastest.
Arguments:
- tokens: bfloat16 [256, 8192], P('gy', 'gx'), may hold values from -6 to 6
- up_old: bfloat16 [8192, 8192], P(('gx', 'gy')), may hold values from -0.0625 to 0.0625
- down_old: bfloat16 [8192, 8192], P(('gx', 'gy')), may hold values from -0.125 to 0.125
- old_slot: int32 [64], replicated, may hold values from 0 to 63, as said below
- new_owner: int32 [64], replicated, may hold values from 0 to 31, as said below
- hot_rank: int32 [64], replicated, may hold values from 0 to 1, as said below
- route: int32 [256], replicated, may hold values from 0 to 255, each once
Outputs:
- up_new: bfloat16 [8192, 8192], P(('gx', 'gy'))
- down_new: bfloat16 [8192, 8192], P(('gx', 'gy'))
- mixed: bfloat16 [256, 8192], P('gy', 'gx')
Inputs may be any that keep to these rules, and one draw needn't show every extreme that they name: `old_slot`: each slot number appears exactly once. `new_owner`: each device index is the new owner of exactly 2 blocks. `hot_rank`: the blocks of one new owner have distinct ranks.
All inputs are finite; a program needn't handle non-finite values.
Results may differ from a plain program's by a relative error of at most 0.0049.
Values may be sent and summed in bfloat16 or wider, within the bound.
No kernel may reach another device: no remote copies, remote signals or barrier semaphores. Data moves between devices by JAX's collectives and lax.ppermute only.
A program may use at most 128 MiB of HBM per device.

v0:
```python
import jax
import jax.numpy as jnp
from jax import lax
from jax.sharding import PartitionSpec as P

BLOCK = 128


def layer_terms(ordered, up_rows, down_rows):
    pre = lax.dot_general(
        ordered, up_rows, (((1,), (1,)), ((), ())), preferred_element_type=jnp.float32
    )
    hidden = jax.nn.gelu(pre, approximate=False).astype(jnp.bfloat16)
    return jnp.dot(hidden, down_rows, preferred_element_type=jnp.float32)


def relocate(up_old, down_old, old_slot, new_owner, hot_rank):
    held = up_old.shape[0] // BLOCK
    width = up_old.shape[1]
    shaped = (up_old.reshape(held, BLOCK, width), down_old.reshape(held, BLOCK, width))
    spread = (
        lax.all_to_all(shaped[0], ("gx", "gy"), split_axis=1, concat_axis=0, tiled=True),
        lax.all_to_all(shaped[1], ("gx", "gy"), split_axis=1, concat_axis=0, tiled=True),
    )
    total = spread[0].shape[0]
    new_slot = new_owner * held + hot_rank
    source = jnp.zeros((total,), jnp.int32).at[new_slot].set(old_slot)
    picked = (jnp.take(spread[0], source, axis=0), jnp.take(spread[1], source, axis=0))
    landed = (
        lax.all_to_all(picked[0], ("gx", "gy"), split_axis=0, concat_axis=1, tiled=True),
        lax.all_to_all(picked[1], ("gx", "gy"), split_axis=0, concat_axis=1, tiled=True),
    )
    return (landed[0].reshape(held * BLOCK, width), landed[1].reshape(held * BLOCK, width))


def shards(tokens, up_old, down_old, old_slot, new_owner, hot_rank, route):
    feature_rows = lax.all_gather(tokens, "gx", axis=1, tiled=True)
    everyone = lax.all_gather(feature_rows, "gy", axis=0, tiled=True)
    ordered = jnp.take(everyone, route, axis=0)
    partial_out = layer_terms(ordered, up_old, down_old)
    up_new, down_new = relocate(up_old, down_old, old_slot, new_owner, hot_rank)
    by_columns = lax.psum_scatter(partial_out, "gx", scatter_dimension=1, tiled=True)
    summed = lax.psum_scatter(by_columns, "gy", scatter_dimension=0, tiled=True)
    return (up_new, down_new, summed.astype(jnp.bfloat16))


def solution(mesh):
    in_specs = (P("gy", "gx"), P(("gx", "gy"), None), P(("gx", "gy"), None), P(), P(), P(), P())
    out_specs = (P(("gx", "gy"), None), P(("gx", "gy"), None), P("gy", "gx"))
    return jax.shard_map(shards, mesh=mesh, in_specs=in_specs, out_specs=out_specs, check_vma=False)
```

profile of v0, /device:TPU:0, one launch (start us, length us, event | category | flops | bytes accessed | tf_op | source)
XLA Modules:
  0.0 539.0 jit_solution(7738522427065044836)
XLA Ops:
  7.2 8.6 %copy.13 = bf16[2,128,8192]{2,0,1:T(2,128)(2,1)} copy(bf16[2,128,8192]{2,1,0:T(8,128)(2,1)} %bitcast.20) | data formatting | bytes 8388608 | tf_op jit(solution)/shard_map/reshape | solution.py:20
  15.7 7.5 %all-to-all-start.2 = ((bf16[2,128,8192]{2,0,1:T(2,128)(2,1)}), bf16[2,128,8192]{2,0,1:T(2,128)(2,1)}, u32[]{:S(2)}, u32[]{:S(2)}) async-start(bf16[2,128,8192]{2,0,1:T(2,128)(2,1)} %copy.13), calls=%async_computation.2 | async-start | bytes 8388608 | tf_op jit(solution)/shard_map/all_to_all | solution.py:23
  23.2 0.0 all-gather.2.cloned.1.call-start
  23.3 29.0 %all_gather.6 = bf16[32,8192]{1,0:T(8,128)(2,1)} all-gather(bf16[32,2048]{1,0:T(8,128)(2,1)S(1)} %copy-done), channel_id=1, replica_groups=mesh['gx'=4,'gy'=8] {'gx'}, dimensions={1}, use_global_device_ids=true | all-gather | bytes 655360 | tf_op jit(solution)/shard_map/all_gather | solution.py:37
  52.2 0.0 all-gather.2.cloned.1.call-update
  52.3 8.6 %copy.10 = bf16[2,128,8192]{2,0,1:T(2,128)(2,1)} copy(bf16[2,128,8192]{2,1,0:T(8,128)(2,1)} %bitcast.19) | data formatting | bytes 8388608 | tf_op jit(solution)/shard_map/reshape | solution.py:20
  60.8 100.0 %all-to-all-done.2 = bf16[2,128,8192]{2,0,1:T(2,128)(2,1)} async-done(((bf16[2,128,8192]{2,0,1:T(2,128)(2,1)}), bf16[2,128,8192]{2,0,1:T(2,128)(2,1)}, u32[]{:S(2)}, u32[]{:S(2)}) %all-to-all-start.2) | async-done | bytes 4194336 | tf_op jit(solution)/shard_map/all_to_all | solution.py:23
  160.9 4.8 all-to-all-start
  165.7 0.5 reduce-scatter.3.cloned.1.call-start
  166.3 8.4 %all-gather.2.cloned.1.call-done = bf16[256,8192]{1,0:T(8,128)(2,1)} async-done(((bf16[32,8192]{1,0:T(8,128)(2,1)}), bf16[256,8192]{1,0:T(8,128)(2,1)}) %all-gather.2.cloned.1.call-update) | async-done | bytes 4194320 | tf_op jit(solution)/shard_map/all_gather | solution.py:38
  174.7 11.7 %gather_fusion = bf16[256,8192]{1,0:T(8,128)(2,1)} fusion(bf16[256,8192]{1,0:T(8,128)(2,1)} %all-gather.2.cloned.1.call-done, s32[1024]{0:T(1024)S(1)} %pad_clamp_fusion), kind=kCustom, calls=%fused_computation.2 | custom fusion | bytes 8389632 | tf_op jit(solution)/shard_map/jit(_take)/gather | solution.py:39
  186.4 13.0 %fusion.17 = f32[256,8192]{1,0:T(8,128)} fusion(bf16[256,8192]{1,0:T(8,128)(2,1)} %param.11, bf16[256,8192]{1,0:T(8,128)(2,1)} %param.10, bf16[256,8192]{1,0:T(8,128)(2,1)} %gather_fusion, pred[256]{0:T(512)(128)(4,1)S(1)} %compare_and_fusion.1), kind=kOutput, calls=%fused_computation.29 | convolution fusion | flops 2153840640 | bytes 20971776 | tf_op jit(solution)/shard_map/dot_general | solution.py:14
  199.4 0.0 reduce-scatter.3.cloned.1.call-update
  199.4 0.6 copy-done.2
  200.1 1.1 scatter_custom_fusion
  201.2 8.8 %copy.14 = bf16[32,2,4,8192]{3,2,1,0:T(4,128)(2,1)} copy(bf16[32,2,4,8192]{3,1,2,0:T(2,128)(2,1)} %bitcast.8) | data formatting | bytes 8388608 | tf_op jit(solution)/shard_map/all_to_all | solution.py:23
  210.0 51.5 %all-to-all-done = bf16[2,128,8192]{2,0,1:T(2,128)(2,1)} async-done(((bf16[2,128,8192]{2,0,1:T(2,128)(2,1)}), bf16[2,128,8192]{2,0,1:T(2,128)(2,1)}, u32[]{:S(2)}, u32[]{:S(2)}) %all-to-all-start) | async-done | bytes 4194336 | tf_op jit(solution)/shard_map/all_to_all | solution.py:22
  261.5 8.1 %copy.11 = bf16[32,2,4,8192]{3,2,1,0:T(4,128)(2,1)} copy(bf16[32,2,4,8192]{3,1,2,0:T(2,128)(2,1)} %bitcast.2) | data formatting | bytes 8388608 | tf_op jit(solution)/shard_map/all_to_all | solution.py:22
  269.6 8.8 %gather_fusion.2 = bf16[64,4,8192]{2,1,0:T(4,128)(2,1)} fusion(bf16[64,4,8192]{2,1,0:T(4,128)(2,1)} %bitcast.22, s32[1024]{0:T(1024)S(1)} %pad_clamp_fusion.1), kind=kCustom, calls=%fused_computation.1.clone | custom fusion | bytes 8388864 | tf_op jit(solution)/shard_map/jit(_take)/gather | solution.py:28
  278.4 8.5 %gather_fusion.1 = bf16[64,4,8192]{2,1,0:T(4,128)(2,1)} fusion(bf16[64,4,8192]{2,1,0:T(4,128)(2,1)} %bitcast.23, s32[1024]{0:T(1024)S(1)} %pad_clamp_fusion.1), kind=kCustom, calls=%fused_computation.clone | custom fusion | bytes 8388864 | tf_op jit(solution)/shard_map/jit(_take)/gather | solution.py:28
  286.9 7.6 %broadcast_select_fusion = (bf16[64,4,8192]{2,1,0:T(4,128)(2,1)S(1)}, bf16[64,4,8192]{2,1,0:T(4,128)(2,1)}) fusion(bf16[64,4,8192]{2,1,0:T(4,128)(2,1)} %gather_fusion.2, pred[64]{0:T(512)(128)(4,1)S(1)} %compare_and_fusion, bf16[64,4,8192]{2,1,0:T(4,128)(2,1)} %gather_fusion.1), kind=kLoop, calls=%fused_computation.6 | loop fusion | flops 4194304 | bytes 16777280 | tf_op jit(solution)/shard_map/jit(_take)/select_n | solution.py:28
  294.6 97.3 %all_to_all.66 = bf16[64,4,8192]{2,1,0:T(4,128)(2,1)} all-to-all(bf16[64,4,8192]{2,1,0:T(4,128)(2,1)S(1)} %get-tuple-element.4), channel_id=1, replica_groups=mesh['gx'=4,'gy'=8] {'gx','gy'}, dimensions={0} | all-to-all | bytes 8388608 | tf_op jit(solution)/shard_map/all_to_all | solution.py:31
  391.9 3.6 all-to-all-start.1
  395.5 0.0 reduce-scatter.5.cloned.1.call-start
  395.5 0.0 reduce-scatter.3.cloned.1.call-done
  395.6 0.7 reduce-scatter.5.cloned.1.call-update
  396.2 7.3 %copy.15 = bf16[2,32,4,8192]{3,2,1,0:T(4,128)(2,1)} copy(bf16[2,32,4,8192]{3,2,0,1:T(4,128)(2,1)} %bitcast.21) | data formatting | bytes 8388608 | tf_op jit(solution)/shard_map/all_to_all | solution.py:31
  403.5 6.9 %reshape.33 = bf16[256,8192]{1,0:T(8,128)(2,1)} reshape(bf16[2,32,4,8192]{3,2,1,0:T(4,128)(2,1)} %copy.15) | data formatting | bytes 8388608 | tf_op jit(solution)/shard_map/reshape | solution.py:33
  410.3 106.2 %all-to-all-done.1 = bf16[64,4,8192]{2,1,0:T(4,128)(2,1)} async-done(((bf16[64,4,8192]{2,1,0:T(4,128)(2,1)}), bf16[64,4,8192]{2,1,0:T(4,128)(2,1)}, u32[]{:S(2)}, u32[]{:S(2)}) %all-to-all-start.1) | async-done | bytes 4194336 | tf_op jit(solution)/shard_map/all_to_all | solution.py:30
  516.5 7.2 %copy.12 = bf16[2,32,4,8192]{3,2,1,0:T(4,128)(2,1)} copy(bf16[2,32,4,8192]{3,2,0,1:T(4,128)(2,1)} %bitcast.5) | data formatting | bytes 8388608 | tf_op jit(solution)/shard_map/all_to_all | solution.py:30
  523.8 6.9 %reshape.31 = bf16[256,8192]{1,0:T(8,128)(2,1)} reshape(bf16[2,32,4,8192]{3,2,1,0:T(4,128)(2,1)} %copy.12) | data formatting | bytes 8388608 | tf_op jit(solution)/shard_map/reshape | solution.py:33
  530.7 1.6 convert_element_type.7
  (15 shorter events, 0.1 us)
Async XLA Ops:
  15.7 7.5 %copy-start = (bf16[32,2048]{1,0:T(8,128)(2,1)S(1)}, bf16[32,2048]{1,0:T(8,128)(2,1)}, u32[]{:S(2)}) copy-start(bf16[32,2048]{1,0:T(8,128)(2,1)} %param.9) | copy-start | bytes 393220
  15.7 145.1 %all-to-all-start.2 = ((bf16[2,128,8192]{2,0,1:T(2,128)(2,1)}), bf16[2,128,8192]{2,0,1:T(2,128)(2,1)}, u32[]{:S(2)}, u32[]{:S(2)}) async-start(bf16[2,128,8192]{2,0,1:T(2,128)(2,1)} %copy.13), calls=%async_computation.2 | async-start | bytes 8388608 | tf_op jit(solution)/shard_map/all_to_all | solution.py:23
  23.2 151.5 %all-gather.2.cloned.1.call-start = ((), (), s32[]{:S(2)}) async-start(), calls=%async_computation.6 | async-start | bytes 4718592 | tf_op jit(solution)/shard_map/all_gather | solution.py:38
  60.8 105.4 %copy-start.1 = (s32[256]{0:T(256)S(1)}, s32[256]{0:T(256)}, u32[]{:S(2)}) copy-start(s32[256]{0:T(256)} %param.15) | copy-start | bytes 3076
  160.9 100.6 %all-to-all-start = ((bf16[2,128,8192]{2,0,1:T(2,128)(2,1)}), bf16[2,128,8192]{2,0,1:T(2,128)(2,1)}, u32[]{:S(2)}, u32[]{:S(2)}) async-start(bf16[2,128,8192]{2,0,1:T(2,128)(2,1)} %copy.10), calls=%async_computation | async-start | bytes 8388608 | tf_op jit(solution)/shard_map/all_to_all | solution.py:22
  165.7 229.8 %reduce-scatter.3.cloned.1.call-start = ((), (), s32[]{:S(2)}) async-start(), calls=%async_computation.7 | async-start | bytes 10485760 | tf_op jit(solution)/shard_map/reduce_scatter | solution.py:42
  199.4 0.7 copy-start.2
  199.4 0.7 copy-start.3
  391.9 124.7 %all-to-all-start.1 = ((bf16[64,4,8192]{2,1,0:T(4,128)(2,1)}), bf16[64,4,8192]{2,1,0:T(4,128)(2,1)}, u32[]{:S(2)}, u32[]{:S(2)}) async-start(bf16[64,4,8192]{2,1,0:T(4,128)(2,1)} %get-tuple-element.5), calls=%async_computation.1 | async-start | bytes 8388608 | tf_op jit(solution)/shard_map/all_to_all | solution.py:30
  395.5 135.2 %reduce-scatter.5.cloned.1.call-start = ((), (), s32[]{:S(2)}) async-start(), calls=%async_computation.8 | async-start | bytes 2359296 | tf_op jit(solution)/shard_map/reduce_scatter | solution.py:43
Sparse Core Ops, SparseCore 0:
  52.4 122.2 all-gather.1
  199.5 77.7 reduce-scatter.2
  399.8 116.0 reduce-scatter.4
where the time goes:
time: 547 us; the launch traced here: 539 us
  waiting for transfers between devices  267 us (49%)
  blocking collectives  126 us (23%)
  local copies, waits for them, and re-layouts  93.1 us (17%)
  starting transfers between devices  16.5 us (3%)
  between operations  14.1 us (3%)
  matrix products  13 us (2%)
  other arithmetic  9.29 us (2%)
    all_to_all x1, waiting for transfers between devices, relocate(): lax.all_to_all(picked[0], ('gx', 'gy'), split_axis=0, concat_axis=1, tile...  106 us
    all_to_all x1, waiting for transfers between devices, relocate(): lax.all_to_all(shaped[1], ('gx', 'gy'), split_axis=1, concat_axis=0, tile...  100 us
    all_to_all x1, blocking collectives, relocate(): lax.all_to_all(picked[1], ('gx', 'gy'), split_axis=0, concat_axis=1, tile...  97.3 us
    all_to_all x1, waiting for transfers between devices, relocate(): lax.all_to_all(shaped[0], ('gx', 'gy'), split_axis=1, concat_axis=0, tile...  51.5 us
    all_gather x1, blocking collectives, shards(): feature_rows = lax.all_gather(tokens, 'gx', axis=1, tiled=True)  29 us
    dot_general x1, matrix products, layer_terms(): return jnp.dot(hidden, down_rows, preferred_element_type=jnp.float32)  13 us
    gather x1, local copies, waits for them, and re-layouts, shards(): ordered = jnp.take(everyone, route, axis=0)  11.7 us
  transfers between devices with their start and end apart: 6, of which 4 were waited for; matrix products, arithmetic and copies ran while one was open for 19% of the time, Pallas kernels for 0%

commit v1 on v0

--- a/solution.py
+++ b/solution.py
@@ -35,7 +35,9 @@
 
 def shards(tokens, up_old, down_old, old_slot, new_owner, hot_rank, route):
     feature_rows = lax.all_gather(tokens, "gx", axis=1, tiled=True)
-    everyone = lax.all_gather(feature_rows, "gy", axis=0, tiled=True)
+    everyone = jnp.concatenate(
+        lax.all_to_all(jnp.stack([feature_rows] * lax.axis_size("gy")), "gy", 0, 0), axis=0
+    )
     ordered = jnp.take(everyone, route, axis=0)
     partial_out = layer_terms(ordered, up_old, down_old)
     up_new, down_new = relocate(up_old, down_old, old_slot, new_owner, hot_rank)

time: 547 us -> 603 us (1.10)
  waiting for transfers between devices: 267 us -> 339 us
  blocking collectives: 126 us -> 106 us
    all_to_all x0 -> x1, waiting for transfers between devices: none -> 85.2 us  [shards(): lax.all_to_all(jnp.stack([feature_rows] * lax.axis_size('gy')), 'gy', 0, 0)]
    all_gather x1, blocking collectives: 29 us -> 8.86 us  [shards(): feature_rows = lax.all_gather(tokens, 'gx', axis=1, tiled=True)]
    all_to_all x1, waiting for transfers between devices: 100 us -> 87.2 us  [relocate(): lax.all_to_all(shaped[1], ('gx', 'gy'), split_axis=1, concat_axis=0, tile...]
    all_to_all x1, waiting for transfers between devices: 51.5 us -> 60.1 us  [relocate(): lax.all_to_all(shaped[0], ('gx', 'gy'), split_axis=1, concat_axis=0, tile...]
    all_gather x1 -> x0, waiting for transfers between devices: 8.39 us -> none  [shards(): everyone = lax.all_gather(feature_rows, 'gy', axis=0, tiled=True)]
where the time goes in v1:
time: 603 us; the launch traced here: 595 us
  waiting for transfers between devices  339 us (56%)
  blocking collectives  106 us (18%)
  local copies, waits for them, and re-layouts  95.4 us (16%)
  starting transfers between devices  17.1 us (3%)
  between operations  14.4 us (2%)
  matrix products  13 us (2%)
  other arithmetic  9.29 us (2%)
    all_to_all x1, waiting for transfers between devices, relocate(): lax.all_to_all(picked[0], ('gx', 'gy'), split_axis=0, concat_axis=1, tile...  106 us
    all_to_all x1, blocking collectives, relocate(): lax.all_to_all(picked[1], ('gx', 'gy'), split_axis=0, concat_axis=1, tile...  97.3 us
    all_to_all x1, waiting for transfers between devices, relocate(): lax.all_to_all(shaped[1], ('gx', 'gy'), split_axis=1, concat_axis=0, tile...  87.2 us
    all_to_all x1, waiting for transfers between devices, shards(): lax.all_to_all(jnp.stack([feature_rows] * lax.axis_size('gy')), 'gy', 0, 0)  85.2 us
    all_to_all x1, waiting for transfers between devices, relocate(): lax.all_to_all(shaped[0], ('gx', 'gy'), split_axis=1, concat_axis=0, tile...  60.1 us
    dot_general x1, matrix products, layer_terms(): return jnp.dot(hidden, down_rows, preferred_element_type=jnp.float32)  13 us
  transfers between devices with their start and end apart: 6, of which 4 were waited for; matrix products, arithmetic and copies ran while one was open for 19% of the time, Pallas kernels for 0%

profile of v1, /device:TPU:0, one launch (start us, length us, event | category | flops | bytes accessed | tf_op | source)
XLA Modules:
  0.0 594.8 jit_solution(5559120070166465609)
XLA Ops:
  7.2 8.9 %all_gather.3 = bf16[32,8192]{1,0:T(8,128)(2,1)S(1)} all-gather(bf16[32,2048]{1,0:T(8,128)(2,1)} %param.9), channel_id=1, replica_groups=mesh['gx'=4,'gy'=8] {'gx'}, dimensions={1}, use_global_device_ids=true | all-gather | bytes 655360 | tf_op jit(solution)/shard_map/all_gather | solution.py:37
  16.0 2.5 stack.2
  18.5 5.8 all-to-all-start.4
  24.4 8.6 %copy.13 = bf16[2,128,8192]{2,0,1:T(2,128)(2,1)} copy(bf16[2,128,8192]{2,1,0:T(8,128)(2,1)} %bitcast.21) | data formatting | bytes 8388608 | tf_op jit(solution)/shard_map/reshape | solution.py:20
  32.9 85.2 %all-to-all-done.4 = bf16[8,32,8192]{2,1,0:T(8,128)(2,1)} async-done(((bf16[8,32,8192]{2,1,0:T(8,128)(2,1)}), bf16[8,32,8192]{2,1,0:T(8,128)(2,1)}, u32[]{:S(2)}, u32[]{:S(2)}) %all-to-all-start.4) | async-done | bytes 4194336 | tf_op jit(solution)/shard_map/all_to_all | solution.py:39
  118.2 3.6 all-to-all-start.2
  121.8 8.6 %copy.10 = bf16[2,128,8192]{2,0,1:T(2,128)(2,1)} copy(bf16[2,128,8192]{2,1,0:T(8,128)(2,1)} %bitcast.20) | data formatting | bytes 8388608 | tf_op jit(solution)/shard_map/reshape | solution.py:20
  130.3 87.2 %all-to-all-done.2 = bf16[2,128,8192]{2,0,1:T(2,128)(2,1)} async-done(((bf16[2,128,8192]{2,0,1:T(2,128)(2,1)}), bf16[2,128,8192]{2,0,1:T(2,128)(2,1)}, u32[]{:S(2)}, u32[]{:S(2)}) %all-to-all-start.2) | async-done | bytes 4194336 | tf_op jit(solution)/shard_map/all_to_all | solution.py:23
  217.5 3.6 all-to-all-start
  221.1 0.5 reduce-scatter.3.cloned.1.call-start
  221.7 11.7 %gather_fusion = bf16[256,8192]{1,0:T(8,128)(2,1)} fusion(bf16[256,8192]{1,0:T(8,128)(2,1)} %bitcast.12, s32[1024]{0:T(1024)S(1)} %pad_clamp_fusion), kind=kCustom, calls=%fused_computation.2 | custom fusion | bytes 8389632 | tf_op jit(solution)/shard_map/jit(_take)/gather | solution.py:41
  233.4 13.0 %fusion.17 = f32[256,8192]{1,0:T(8,128)} fusion(bf16[256,8192]{1,0:T(8,128)(2,1)} %param.11, bf16[256,8192]{1,0:T(8,128)(2,1)} %param.10, bf16[256,8192]{1,0:T(8,128)(2,1)} %gather_fusion, pred[256]{0:T(512)(128)(4,1)S(1)} %compare_and_fusion.1), kind=kOutput, calls=%fused_computation.29 | convolution fusion | flops 2153840640 | bytes 20971776 | tf_op jit(solution)/shard_map/dot_general | solution.py:14
  246.4 0.0 reduce-scatter.3.cloned.1.call-update
  246.4 0.6 copy-done.1
  247.1 1.1 scatter_custom_fusion
  248.2 8.7 %copy.14 = bf16[32,2,4,8192]{3,2,1,0:T(4,128)(2,1)} copy(bf16[32,2,4,8192]{3,1,2,0:T(2,128)(2,1)} %bitcast.8) | data formatting | bytes 8388608 | tf_op jit(solution)/shard_map/all_to_all | solution.py:23
  256.8 60.1 %all-to-all-done = bf16[2,128,8192]{2,0,1:T(2,128)(2,1)} async-done(((bf16[2,128,8192]{2,0,1:T(2,128)(2,1)}), bf16[2,128,8192]{2,0,1:T(2,128)(2,1)}, u32[]{:S(2)}, u32[]{:S(2)}) %all-to-all-start) | async-done | bytes 4194336 | tf_op jit(solution)/shard_map/all_to_all | solution.py:22
  316.9 8.1 %copy.11 = bf16[32,2,4,8192]{3,2,1,0:T(4,128)(2,1)} copy(bf16[32,2,4,8192]{3,1,2,0:T(2,128)(2,1)} %bitcast.2) | data formatting | bytes 8388608 | tf_op jit(solution)/shard_map/all_to_all | solution.py:22
  325.1 8.8 %gather_fusion.2 = bf16[64,4,8192]{2,1,0:T(4,128)(2,1)} fusion(bf16[64,4,8192]{2,1,0:T(4,128)(2,1)} %bitcast.23, s32[1024]{0:T(1024)S(1)} %pad_clamp_fusion.1), kind=kCustom, calls=%fused_computation.1.clone | custom fusion | bytes 8388864 | tf_op jit(solution)/shard_map/jit(_take)/gather | solution.py:28
  333.8 8.5 %gather_fusion.1 = bf16[64,4,8192]{2,1,0:T(4,128)(2,1)} fusion(bf16[64,4,8192]{2,1,0:T(4,128)(2,1)} %bitcast.24, s32[1024]{0:T(1024)S(1)} %pad_clamp_fusion.1), kind=kCustom, calls=%fused_computation.clone | custom fusion | bytes 8388864 | tf_op jit(solution)/shard_map/jit(_take)/gather | solution.py:28
  342.4 7.6 %broadcast_select_fusion = (bf16[64,4,8192]{2,1,0:T(4,128)(2,1)S(1)}, bf16[64,4,8192]{2,1,0:T(4,128)(2,1)}) fusion(bf16[64,4,8192]{2,1,0:T(4,128)(2,1)} %gather_fusion.2, pred[64]{0:T(512)(128)(4,1)S(1)} %compare_and_fusion, bf16[64,4,8192]{2,1,0:T(4,128)(2,1)} %gather_fusion.1), kind=kLoop, calls=%fused_computation.6 | loop fusion | flops 4194304 | bytes 16777280 | tf_op jit(solution)/shard_map/jit(_take)/select_n | solution.py:28
  350.0 97.3 %all_to_all.71 = bf16[64,4,8192]{2,1,0:T(4,128)(2,1)} all-to-all(bf16[64,4,8192]{2,1,0:T(4,128)(2,1)S(1)} %get-tuple-element.4), channel_id=1, replica_groups=mesh['gx'=4,'gy'=8] {'gx','gy'}, dimensions={0} | all-to-all | bytes 8388608 | tf_op jit(solution)/shard_map/all_to_all | solution.py:31
  447.3 3.6 all-to-all-start.1
  450.9 0.0 reduce-scatter.5.cloned.1.call-start
  451.0 0.0 reduce-scatter.3.cloned.1.call-done
  451.0 0.7 reduce-scatter.5.cloned.1.call-update
  451.7 7.2 %copy.15 = bf16[2,32,4,8192]{3,2,1,0:T(4,128)(2,1)} copy(bf16[2,32,4,8192]{3,2,0,1:T(4,128)(2,1)} %bitcast.22) | data formatting | bytes 8388608 | tf_op jit(solution)/shard_map/all_to_all | solution.py:31
  458.9 6.9 %reshape.38 = bf16[256,8192]{1,0:T(8,128)(2,1)} reshape(bf16[2,32,4,8192]{3,2,1,0:T(4,128)(2,1)} %copy.15) | data formatting | bytes 8388608 | tf_op jit(solution)/shard_map/reshape | solution.py:33
  465.8 106.2 %all-to-all-done.1 = bf16[64,4,8192]{2,1,0:T(4,128)(2,1)} async-done(((bf16[64,4,8192]{2,1,0:T(4,128)(2,1)}), bf16[64,4,8192]{2,1,0:T(4,128)(2,1)}, u32[]{:S(2)}, u32[]{:S(2)}) %all-to-all-start.1) | async-done | bytes 4194336 | tf_op jit(solution)/shard_map/all_to_all | solution.py:30
  572.0 7.2 %copy.12 = bf16[2,32,4,8192]{3,2,1,0:T(4,128)(2,1)} copy(bf16[2,32,4,8192]{3,2,0,1:T(4,128)(2,1)} %bitcast.5) | data formatting | bytes 8388608 | tf_op jit(solution)/shard_map/all_to_all | solution.py:30
  579.2 6.9 %reshape.36 = bf16[256,8192]{1,0:T(8,128)(2,1)} reshape(bf16[2,32,4,8192]{3,2,1,0:T(4,128)(2,1)} %copy.12) | data formatting | bytes 8388608 | tf_op jit(solution)/shard_map/reshape | solution.py:33
  586.1 1.6 convert_element_type.7
  (13 shorter events, 0.1 us)
Async XLA Ops:
  18.5 99.6 %all-to-all-start.4 = ((bf16[8,32,8192]{2,1,0:T(8,128)(2,1)}), bf16[8,32,8192]{2,1,0:T(8,128)(2,1)}, u32[]{:S(2)}, u32[]{:S(2)}) async-start(bf16[8,32,8192]{2,1,0:T(8,128)(2,1)} %stack.2), calls=%async_computation.4 | async-start | bytes 8388608 | tf_op jit(solution)/shard_map/all_to_all | solution.py:39
  118.2 99.4 %all-to-all-start.2 = ((bf16[2,128,8192]{2,0,1:T(2,128)(2,1)}), bf16[2,128,8192]{2,0,1:T(2,128)(2,1)}, u32[]{:S(2)}, u32[]{:S(2)}) async-start(bf16[2,128,8192]{2,0,1:T(2,128)(2,1)} %copy.13), calls=%async_computation.2 | async-start | bytes 8388608 | tf_op jit(solution)/shard_map/all_to_all | solution.py:23
  130.3 91.3 %copy-start = (s32[256]{0:T(256)S(1)}, s32[256]{0:T(256)}, u32[]{:S(2)}) copy-start(s32[256]{0:T(256)} %param.15) | copy-start | bytes 3076
  217.5 99.4 %all-to-all-start = ((bf16[2,128,8192]{2,0,1:T(2,128)(2,1)}), bf16[2,128,8192]{2,0,1:T(2,128)(2,1)}, u32[]{:S(2)}, u32[]{:S(2)}) async-start(bf16[2,128,8192]{2,0,1:T(2,128)(2,1)} %copy.10), calls=%async_computation | async-start | bytes 8388608 | tf_op jit(solution)/shard_map/all_to_all | solution.py:22
  221.1 229.9 %reduce-scatter.3.cloned.1.call-start = ((), (), s32[]{:S(2)}) async-start(), calls=%async_computation.7 | async-start | bytes 10485760 | tf_op jit(solution)/shard_map/reduce_scatter | solution.py:44
  246.4 0.7 copy-start.1
  246.4 0.7 copy-start.2
  447.3 124.7 %all-to-all-start.1 = ((bf16[64,4,8192]{2,1,0:T(4,128)(2,1)}), bf16[64,4,8192]{2,1,0:T(4,128)(2,1)}, u32[]{:S(2)}, u32[]{:S(2)}) async-start(bf16[64,4,8192]{2,1,0:T(4,128)(2,1)} %get-tuple-element.5), calls=%async_computation.1 | async-start | bytes 8388608 | tf_op jit(solution)/shard_map/all_to_all | solution.py:30
  450.9 135.2 %reduce-scatter.5.cloned.1.call-start = ((), (), s32[]{:S(2)}) async-start(), calls=%async_computation.8 | async-start | bytes 2359296 | tf_op jit(solution)/shard_map/reduce_scatter | solution.py:45
Sparse Core Ops, SparseCore 0:
  246.5 83.3 reduce-scatter.2
  455.3 116.0 reduce-scatter.4
